TPU v7x, 32 devices: a whole 2x2x4 slice. The times are simulated.
32 devices in a mesh: dp: 8 (over z, x), feat: 4 (over y, core).
Axes of the slice: x: 2, y: 2, z: 4, core: 2. Of those that a mesh axis runs over, the one named last changes fastest.
Arguments:
- features: float32 [24576, 2048], P('dp', 'feat'), may hold values from -200 to 200
- gamma: float32 [2048], P('feat'), may hold values from 0.5 to 1.5
- beta: float32 [2048], P('feat'), may hold values from -3 to 3
- weight: bfloat16 [2048, 2048], P(None, 'feat'), may hold values from -0.125 to 0.125
- bias: float32 [2048], P('feat'), may hold values from -3 to 3
Outputs:
- activated: float32 [24576, 2048], P('dp', 'feat')
All inputs are finite; a program needn't handle non-finite values.
Results may differ from a plain program's by a relative error of at most 0.0026.
Values may be sent and summed in bfloat16 or wider, within the bound.
No kernel may reach another device: no remote copies, remote signals or barrier semaphores. Data moves between devices by JAX's collectives and lax.ppermute only.
A program may use at most 128 MiB of HBM per device.

v0:
```python
import functools

import jax
import jax.numpy as jnp
from jax import lax
from jax.experimental import pallas as pl
from jax.experimental.pallas import tpu as pltpu
from jax.sharding import PartitionSpec as P


UNITS = 96
EARLY = (8, 24)
LATE = (28, 16, 9, 5, 4)
DIRECT = 2
PIECE = 12
SPLIT = 3


def grant(kib):
    return pltpu.CompilerParams(vmem_limit_bytes=kib * 1024)


def centre_kernel(x_ref, sent_ref, mean_ref, buf, sem):
    copy = pltpu.make_async_copy(x_ref.at[pl.ds(0, buf.shape[0]), :], buf, sem)
    copy.start()
    copy.wait()
    x = buf[...]
    mean = jnp.mean(x, axis=0, keepdims=True)
    sent_ref[...] = (x - mean).astype(jnp.bfloat16)
    mean_ref[...] = mean


def centre(features, count):
    cols = features.shape[1]
    return pl.pallas_call(
        centre_kernel,
        in_specs=[pl.BlockSpec(memory_space=pltpu.HBM)],
        out_specs=[pl.BlockSpec(memory_space=pltpu.VMEM)] * 2,
        out_shape=[
            jax.ShapeDtypeStruct((count, cols), jnp.bfloat16),
            jax.ShapeDtypeStruct((1, cols), jnp.float32),
        ],
        scratch_shapes=[pltpu.VMEM((count, cols), jnp.float32), pltpu.SemaphoreType.DMA],
        compiler_params=grant(51000),
    )(features)


def survey_kernel(x_ref, pivot_ref, held_ref, sent_ref, means_ref, total_ref, sems, *, early, others):
    rows, cols = held_ref.shape
    copies = []
    for p, (start, size) in enumerate(early + others):
        place = pl.ds(start, size)
        copies.append(pltpu.make_async_copy(x_ref.at[place, :], held_ref.at[place, :], sems.at[p]))
        copies[-1].start()
    pivot = pivot_ref[...]
    groups = []
    for p, (start, size) in enumerate(early):
        copies[p].wait()
        x = held_ref[pl.ds(start, size), :]
        mean = jnp.mean(x, axis=0, keepdims=True)
        d = x - mean
        sent_ref[pl.ds(start - early[0][0], size), :] = d.astype(jnp.bfloat16)
        means_ref[pl.ds(p, 1), :] = mean
        groups.append((size, mean, jnp.sum(d * d, axis=0, keepdims=True)))
    sums = jnp.zeros((8, cols), jnp.float32)
    devs = jnp.zeros((8, cols), jnp.float32)
    rest = 0
    for p, (start, size) in enumerate(others, len(early)):
        copies[p].wait()
        d = (held_ref[pl.ds(start, size), :] - pivot).reshape(-1, 8, cols)
        sums = sums + jnp.sum(d, axis=0)
        devs = devs + jnp.sum(d * d, axis=0)
        rest += size
    shift = jnp.sum(sums, axis=0, keepdims=True) / rest
    dev = jnp.sum(devs, axis=0, keepdims=True) - rest * (shift * shift)
    groups.append((rest, pivot + shift, dev))
    mean = sum(n * m for n, m, _ in groups) / rows
    dev = sum(d + n * ((m - mean) * (m - mean)) for n, m, d in groups)
    total_ref[0:1, :] = mean
    total_ref[1:2, :] = dev


def survey(features, pivot, first, early, piece):
    rows, cols = features.shape
    pieces = tuple((first + p, piece) for p in range(0, early, piece))
    others = tuple((p, min(2 * piece, rows - p)) for p in range(first + early, rows, 2 * piece)) + ((0, first),)
    return pl.pallas_call(
        functools.partial(survey_kernel, early=pieces, others=others),
        in_specs=[pl.BlockSpec(memory_space=pltpu.HBM), pl.BlockSpec(memory_space=pltpu.VMEM)],
        out_specs=[pl.BlockSpec(memory_space=pltpu.VMEM)] * 4,
        out_shape=[
            jax.ShapeDtypeStruct((rows, cols), jnp.float32),
            jax.ShapeDtypeStruct((early, cols), jnp.bfloat16),
            jax.ShapeDtypeStruct((early // piece, cols), jnp.float32),
            jax.ShapeDtypeStruct((2, cols), jnp.float32),
        ],
        scratch_shapes=[pltpu.SemaphoreType.DMA((len(pieces) + len(others),))],
        compiler_params=grant(46000),
    )(features, pivot)


def shard_order():
    feat = lax.axis_size("feat")
    me = lax.axis_index("feat")
    order = [me, me ^ 1]
    for s in range(2, feat, 2):
        source = (me - s) % feat
        order += [source, source ^ 1]
    return order


def weights_of(w_ref, place, cols):
    return w_ref[pl.ds(pl.multiple_of(shard_order()[place] * cols, cols), cols), :]


def product(xs, places, w_ref, total):
    for x, place in zip(xs, places):
        w = weights_of(w_ref, place, x.shape[1])
        total = total + jnp.dot(x, w, preferred_element_type=jnp.float32)
    return total


def part_kernel(*refs, places):
    n = len(places)
    xs, (w_ref, bias_ref, out_ref) = refs[:n], refs[n:]
    out_ref[...] = product([x[...] for x in xs], places, w_ref, bias_ref[...])


def part(xs, places, weight, bias):
    return pl.pallas_call(
        functools.partial(part_kernel, places=places),
        in_specs=[pl.BlockSpec(memory_space=pltpu.VMEM)] * (len(xs) + 2),
        out_specs=pl.BlockSpec(memory_space=pltpu.VMEM),
        out_shape=jax.ShapeDtypeStruct((xs[0].shape[0], weight.shape[1]), jnp.float32),
        compiler_params=grant(12288),
    )(*xs, weight, bias)


def layer_kernel(*refs, places, first, blocks):
    n = len(places)
    xs, (w_ref, base_ref) = refs[:n], refs[n : n + 2]
    out_ref, buf, sems = refs[-3:]
    copies = []
    for b, (start, size) in enumerate(blocks):
        rows = pl.ds(start, size)
        base = base_ref[...] if base_ref.shape[0] == 1 else base_ref[rows, :]
        buf[rows, :] = jnp.maximum(product([x[rows, :] for x in xs], places, w_ref, base), 0.0)
        copies.append(pltpu.make_async_copy(buf.at[rows, :], out_ref.at[pl.ds(first + start, size), :], sems.at[b]))
        copies[-1].start()
    for copy in copies:
        copy.wait()


def layer(xs, places, weight, base, out, first, rows):
    count = xs[0].shape[0]
    width = weight.shape[1]
    blocks = tuple((start, min(256, count - start)) for start in range(0, count, 256))
    in_specs = [pl.BlockSpec(memory_space=pltpu.VMEM)] * (len(xs) + 2)
    args = [*xs, weight, base]
    aliases = {}
    if out is not None:
        in_specs += [pl.BlockSpec(memory_space=pltpu.HBM)]
        aliases = {len(args): 0}
        args += [out]
    return pl.pallas_call(
        functools.partial(layer_kernel, places=places, first=first, blocks=blocks),
        in_specs=in_specs,
        out_specs=pl.BlockSpec(memory_space=pltpu.HBM),
        out_shape=jax.ShapeDtypeStruct((rows, width), jnp.float32),
        input_output_aliases=aliases,
        scratch_shapes=[pltpu.VMEM((count, width), jnp.float32), pltpu.SemaphoreType.DMA((len(blocks),))],
        compiler_params=grant(12288),
    )(*args)


def finish_kernel(*refs, shifts):
    passed, far, cross = refs[:shifts], refs[shifts : 2 * shifts], refs[2 * shifts : 3 * shifts]
    w_ref, base_ref, tail_ref, _, out_ref, buf, sem = refs[3 * shifts :]
    count = buf.shape[0]
    tail = product([x[...] for x in far], range(2, 2 + 2 * shifts, 2), w_ref, tail_ref[...])
    xs = [jnp.concatenate([p[...], c[...]]) for p, c in zip(passed, cross)]
    base = jnp.concatenate([base_ref[...], tail])
    buf[...] = jnp.maximum(product(xs, range(3, 3 + 2 * shifts, 2), w_ref, base), 0.0)
    copy = pltpu.make_async_copy(buf, out_ref.at[pl.ds(out_ref.shape[0] - count, count), :], sem)
    copy.start()
    copy.wait()


def finish(passed, far, cross, weight, base, tail, out):
    count = base.shape[0] + tail.shape[0]
    vmem = 3 * len(passed) + 3
    return pl.pallas_call(
        functools.partial(finish_kernel, shifts=len(passed)),
        in_specs=[pl.BlockSpec(memory_space=pltpu.VMEM)] * vmem + [pl.BlockSpec(memory_space=pltpu.HBM)],
        out_specs=pl.BlockSpec(memory_space=pltpu.HBM),
        out_shape=jax.ShapeDtypeStruct(out.shape, out.dtype),
        input_output_aliases={vmem: 0},
        scratch_shapes=[pltpu.VMEM((count, weight.shape[1]), jnp.float32), pltpu.SemaphoreType.DMA],
        compiler_params=grant(12288),
    )(*passed, *far, *cross, weight, base, tail, out)


def local(features, gamma, beta, weight, bias):
    rows, cols = features.shape
    dp = lax.axis_size("dp")
    feat = lax.axis_size("feat")
    unit = rows // UNITS
    total_rows = rows * dp
    near = [(i, i ^ 1) for i in range(feat)]
    shifts = range(2, feat, 2)

    def to_far(x):
        return [lax.ppermute(x, "feat", [(i, (i + s) % feat) for i in range(feat)]) for s in shifts]

    def to_cross(x):
        return [lax.ppermute(x, "feat", [(i, (i + s) % feat ^ 1) for i in range(feat)]) for s in shifts]

    def to_near(x):
        return lax.ppermute(x, "feat", near)

    firsts = [0]
    for count in EARLY + LATE + (DIRECT,):
        firsts.append(firsts[-1] + count)
    piece = PIECE * unit
    sizes = [EARLY[0] * unit, piece]
    sent, pivot = centre(features, EARLY[0] * unit)
    early = [to_far(sent)]
    features, sent, means, mine = survey(features, pivot, EARLY[0] * unit, EARLY[1] * unit, piece)
    early.append(to_far(sent))
    found = [pivot, means]
    step, held = 1, rows
    while step < dp:
        theirs = lax.ppermute(mine, "dp", [(i, i ^ step) for i in range(dp)])
        gap = mine[0] - theirs[0]
        mean = (mine[0] + theirs[0]) * 0.5
        dev = mine[1] + theirs[1] + (0.5 * held) * (gap * gap)
        mine = jnp.stack([mean, dev])
        step, held = 2 * step, 2 * held
    mean = mine[0]
    var = mine[1] / total_rows
    scale = gamma / jnp.sqrt(var + 1e-05)

    def normalize(k):
        x = features[firsts[k] * unit : firsts[k + 1] * unit]
        return ((x - mean) * scale + beta).astype(jnp.bfloat16)

    own, arrived = {}, {}
    last = len(EARLY) + len(LATE)
    for k in range(len(EARLY), last + 1):
        own[k] = normalize(k)
        arrived[k] = to_far(own[k])
    crossed = to_cross(own[last])
    offsets = (jnp.concatenate(found) - mean) * scale + beta
    table = to_far(jnp.concatenate([scale[None], offsets]))
    row = 1
    for k, means in enumerate(found):
        own[k] = normalize(k)
        arrived[k] = []
        blocks = means.shape[0]
        for got, t in zip(early[k], table):
            got = got.reshape(blocks, sizes[k], cols).astype(jnp.float32)
            got = got * t[0] + t[row : row + blocks][:, None, :]
            arrived[k].append(got.astype(jnp.bfloat16).reshape(blocks * sizes[k], cols))
        row += blocks

    out = None
    bias = bias[None]
    places = tuple(range(2 + 2 * len(shifts)))
    xs = [own[last], to_near(own[last])]
    tail = part(xs, places[:2], weight, bias)
    for k in range(last):
        xs = {0: own[k], 1: to_near(own[k])}
        for place, got in zip(places[2::2], arrived[k]):
            xs[place], xs[place + 1] = got, to_near(got)
        wanted, base = places, bias
        if k >= last - SPLIT:
            wanted = places[3::2]
            held = tuple(p for p in places if p not in wanted)
            base = part([xs[p] for p in held], held, weight, bias)
        xs = [xs[p] for p in wanted]
        if k < last - 1:
            out = layer(xs, wanted, weight, base, out, firsts[k] * unit, rows)
    return finish(xs, arrived[last], crossed, weight, base, tail, out)


def solution(mesh):
    placed = (P("dp", "feat"), P("feat"), P("feat"), P(None, "feat"), P("feat"))
    return jax.shard_map(local, mesh=mesh, in_specs=placed, out_specs=P("dp", "feat"), check_vma=False)
```

profile of v0, /device:TPU:0, one launch (start us, length us, event | category | flops | bytes accessed | tf_op | source)
XLA Modules:
  0.0 103.6 jit_solution(13748845043620758440)
XLA Ops:
  0.0 1.1 %shard_map.55 = (bf16[256,512]{1,0:T(8,128)(2,1)S(1)}, f32[1,512]{1,0:T(1,128)S(1)}) custom-call(f32[3072,512]{1,0:T(8,128)} %x_ref.3), custom_call_target="tpu_custom_call" | custom-call | tf_op jit(solution)/shard_map/pallas_call | solution.py:35
  1.2 3.0 %shard_map.56 = (f32[3072,512]{1,0:T(8,128)S(1)}, bf16[768,512]{1,0:T(8,128)(2,1)S(1)}, f32[2,512]{1,0:T(2,128)S(1)}, f32[2,512]{1,0:T(2,128)S(1)}) custom-call(f32[3072,512]{1,0:T(8,128)} %x_ref.3, f32[1,512]{1,0:T(1,128)S(1)} %get-tuple-element.11.pivot_ref), custom_call_target="tpu_custom_call" | custom-call | tf_op jit(solution)/shard_map/pallas_call | solution.py:87
  4.2 3.0 %collective-permute-start = (f32[2,512]{1,0:T(2,128)S(1)}, f32[2,512]{1,0:T(2,128)S(1)}, u32[]{:S(2)}, u32[]{:S(2)}) collective-permute-start(f32[2,512]{1,0:T(2,128)S(1)} %get-tuple-element.13), channel_id=1, source_target_pairs={{0,4},{4,0},{8,12},{12,8},{16,20},{20,16},{24,28},{28,24},{1,5},{5... | collective-permute-start | bytes 12296 | tf_op jit(solution)/shard_map/ppermute | solution.py:233
  7.2 1.6 %collective-permute-done = f32[2,512]{1,0:T(2,128)S(1)} collective-permute-done((f32[2,512]{1,0:T(2,128)S(1)}, f32[2,512]{1,0:T(2,128)S(1)}, u32[]{:S(2)}, u32[]{:S(2)}) %collective-permute-start) | collective-permute-done | bytes 4128 | tf_op jit(solution)/shard_map/ppermute | solution.py:233
  8.8 2.2 %collective-permute-start.1 = (f32[2,512]{1,0:T(2,128)S(1)}, f32[2,512]{1,0:T(2,128)S(1)}, u32[]{:S(2)}, u32[]{:S(2)}) collective-permute-start(f32[2,512]{1,0:T(2,128)S(1)} %pad_maximum_fusion.1), channel_id=1, source_target_pairs={{0,8},{4,12},{8,0},{12,4},{16,24},{20,28},{24,16},{28,20},{1,9},{5... | collective-permute-start | bytes 12296 | tf_op jit(solution)/shard_map/ppermute | solution.py:233
  11.0 1.6 %collective-permute-done.1 = f32[2,512]{1,0:T(2,128)S(1)} collective-permute-done((f32[2,512]{1,0:T(2,128)S(1)}, f32[2,512]{1,0:T(2,128)S(1)}, u32[]{:S(2)}, u32[]{:S(2)}) %collective-permute-start.1) | collective-permute-done | bytes 4128 | tf_op jit(solution)/shard_map/ppermute | solution.py:233
  12.6 3.1 %collective-permute-start.2 = (f32[2,512]{1,0:T(2,128)S(1)}, f32[2,512]{1,0:T(2,128)S(1)}, u32[]{:S(2)}, u32[]{:S(2)}) collective-permute-start(f32[2,512]{1,0:T(2,128)S(1)} %pad_maximum_fusion.2), channel_id=1, source_target_pairs={{0,16},{4,20},{8,24},{12,28},{16,0},{20,4},{24,8},{28,12},{1,17},{... | collective-permute-start | bytes 12296 | tf_op jit(solution)/shard_map/ppermute | solution.py:233
  15.7 1.5 %collective-permute-start.26 = (bf16[256,512]{1,0:T(8,128)(2,1)S(1)}, bf16[256,512]{1,0:T(8,128)(2,1)S(1)}, u32[]{:S(2)}, u32[]{:S(2)}) collective-permute-start(bf16[256,512]{1,0:T(8,128)(2,1)S(1)} %get-tuple-element.16), channel_id=1, source_target_pairs={{0,2},{1,3},{2,0},{3,1},{4,6},{5,7},{6,4},{7,5},{8,10},{9,11},{10,... | collective-permute-start | bytes 786440 | tf_op jit(solution)/shard_map/ppermute | solution.py:213
  17.9 1.9 %collective-permute-start.23 = (f32[4,512]{1,0:T(4,128)S(1)}, f32[4,512]{1,0:T(4,128)S(1)}, u32[]{:S(2)}, u32[]{:S(2)}) collective-permute-start(f32[4,512]{1,0:T(4,128)S(1)} %pad_maximum_fusion), channel_id=1, source_target_pairs={{0,2},{1,3},{2,0},{3,1},{4,6},{5,7},{6,4},{7,5},{8,10},{9,11},{10,... | collective-permute-start | bytes 24584 | tf_op jit(solution)/shard_map/ppermute | solution.py:213
  20.6 2.3 %collective-permute-done.23 = f32[4,512]{1,0:T(4,128)S(1)} collective-permute-done((f32[4,512]{1,0:T(4,128)S(1)}, f32[4,512]{1,0:T(4,128)S(1)}, u32[]{:S(2)}, u32[]{:S(2)}) %collective-permute-start.23) | collective-permute-done | bytes 8224 | tf_op jit(solution)/shard_map/ppermute | solution.py:213
  23.0 1.2 %collective-permute-done.8.refs_1_ = bf16[64,512]{1,0:T(8,128)(2,1)S(1)} collective-permute-done((bf16[64,512]{1,0:T(8,128)(2,1)S(1)}, bf16[64,512]{1,0:T(8,128)(2,1)S(1)}, u32[]{:S(2)}, u32[]{:S(2)}) %collective-permute-start.8) | collective-permute-done | bytes 65568 | tf_op jit(solution)/shard_map/ppermute | solution.py:219
  24.2 1.4 %collective-permute-start.22 = (bf16[768,512]{1,0:T(8,128)(2,1)S(1)}, bf16[768,512]{1,0:T(8,128)(2,1)S(1)}, u32[]{:S(2)}, u32[]{:S(2)}) collective-permute-start(bf16[768,512]{1,0:T(8,128)(2,1)S(1)} %get-tuple-element.14), channel_id=1, source_target_pairs={{0,2},{1,3},{2,0},{3,1},{4,6},{5,7},{6,4},{7,5},{8,10},{9,11},{10,... | collective-permute-start | bytes 2359304 | tf_op jit(solution)/shard_map/ppermute | solution.py:213
  25.5 0.7 collective-permute-start.9
  26.2 1.4 %collective-permute-start.19 = (bf16[896,512]{1,0:T(8,128)(2,1)S(1)}, bf16[896,512]{1,0:T(8,128)(2,1)S(1)}, u32[]{:S(2)}, u32[]{:S(2)}) collective-permute-start(bf16[896,512]{1,0:T(8,128)(2,1)S(1)} %add_convert_fusion.refs_0_), channel_id=1, source_target_pairs={{0,2},{1,3},{2,0},{3,1},{4,6},{5,7},{6,4},{7,5},{8,10},{9,11},{10,... | collective-permute-start | bytes 2752520 | tf_op jit(solution)/shard_map/ppermute | solution.py:213
  27.7 20.4 %collective-permute-done.9.refs_2_ = bf16[160,512]{1,0:T(8,128)(2,1)S(1)} collective-permute-done((bf16[160,512]{1,0:T(8,128)(2,1)S(1)}, bf16[160,512]{1,0:T(8,128)(2,1)S(1)}, u32[]{:S(2)}, u32[]{:S(2)}) %collective-permute-start.9) | collective-permute-done | bytes 163872 | tf_op jit(solution)/shard_map/ppermute | solution.py:213
  48.1 1.4 %collective-permute-start.12 = (bf16[288,512]{1,0:T(8,128)(2,1)S(1)}, bf16[288,512]{1,0:T(8,128)(2,1)S(1)}, u32[]{:S(2)}, u32[]{:S(2)}) collective-permute-start(bf16[288,512]{1,0:T(8,128)(2,1)S(1)} %add_convert_fusion.3.refs_0_), channel_id=1, source_target_pairs={{0,2},{1,3},{2,0},{3,1},{4,6},{5,7},{6,4},{7,5},{8,10},{9,11},{10,... | collective-permute-start | bytes 884744 | tf_op jit(solution)/shard_map/ppermute | solution.py:213
  49.5 0.7 collective-permute-start.16
  50.3 23.8 %collective-permute-done.12.refs_2_ = bf16[288,512]{1,0:T(8,128)(2,1)S(1)} collective-permute-done((bf16[288,512]{1,0:T(8,128)(2,1)S(1)}, bf16[288,512]{1,0:T(8,128)(2,1)S(1)}, u32[]{:S(2)}, u32[]{:S(2)}) %collective-permute-start.12) | collective-permute-done | bytes 294944 | tf_op jit(solution)/shard_map/ppermute | solution.py:213
  74.1 0.5 collective-permute-start.27
  74.8 1.5 %collective-permute-done.27.refs_3_ = bf16[256,512]{1,0:T(8,128)(2,1)S(1)} collective-permute-done((bf16[256,512]{1,0:T(8,128)(2,1)S(1)}, bf16[256,512]{1,0:T(8,128)(2,1)S(1)}, u32[]{:S(2)}, u32[]{:S(2)}) %collective-permute-start.27) | collective-permute-done | bytes 262176 | tf_op jit(solution)/shard_map/ppermute | solution.py:219
  77.2 7.3 %collective-permute-done.16.refs_2_ = bf16[512,512]{1,0:T(8,128)(2,1)S(1)} collective-permute-done((bf16[512,512]{1,0:T(8,128)(2,1)S(1)}, bf16[512,512]{1,0:T(8,128)(2,1)S(1)}, u32[]{:S(2)}, u32[]{:S(2)}) %collective-permute-start.16) | collective-permute-done | bytes 524320 | tf_op jit(solution)/shard_map/ppermute | solution.py:213
  84.5 0.5 collective-permute-start.17
  85.5 2.0 %collective-permute-done.17.refs_3_ = bf16[512,512]{1,0:T(8,128)(2,1)S(1)} collective-permute-done((bf16[512,512]{1,0:T(8,128)(2,1)S(1)}, bf16[512,512]{1,0:T(8,128)(2,1)S(1)}, u32[]{:S(2)}, u32[]{:S(2)}) %collective-permute-start.17) | collective-permute-done | bytes 524320 | tf_op jit(solution)/shard_map/ppermute | solution.py:219
  87.7 1.4 %collective-permute-start.5 = (bf16[64,512]{1,0:T(8,128)(2,1)S(1)}, bf16[64,512]{1,0:T(8,128)(2,1)S(1)}, u32[]{:S(2)}, u32[]{:S(2)}) collective-permute-start(bf16[64,512]{1,0:T(8,128)(2,1)S(1)} %add_convert_fusion.8.refs_0_), channel_id=1, source_target_pairs={{0,2},{1,3},{2,0},{3,1},{4,6},{5,7},{6,4},{7,5},{8,10},{9,11},{10,... | collective-permute-start | bytes 196616 | tf_op jit(solution)/shard_map/ppermute | solution.py:213
  90.5 0.6 shard_map.60.refs_2_
  91.2 1.5 %shard_map.61.refs_6_ = f32[3072,512]{1,0:T(8,128)} custom-call(bf16[256,512]{1,0:T(8,128)(2,1)S(1)} %add_convert_fusion.5.refs_0_, bf16[256,512]{1,0:T(8,128)(2,1)S(1)} %collective-permute-done.25.refs_1_, bf16[256,512]{1,0:T(8,128)(2,1)S(1)} %add_convert_fusion.4.refs_2_, bf16[256,512]{1,0:T(8,128)(2,1)S(1)} %collective-permute-done.27.refs_3_, ...), custom_call_target="tpu_custom_call" | custom-call | tf_op jit(solution)/shard_map/pallas_call | solution.py:165
  92.7 2.6 %shard_map.62.refs_6_ = f32[3072,512]{1,0:T(8,128)} custom-call(bf16[768,512]{1,0:T(8,128)(2,1)S(1)} %add_convert_fusion.1.refs_0_, bf16[768,512]{1,0:T(8,128)(2,1)S(1)} %collective-permute-done.21.refs_1_, bf16[768,512]{1,0:T(8,128)(2,1)S(1)} %fusion.refs_2_, bf16[768,512]{1,0:T(8,128)(2,1)S(1)} %collective-permute-done.24.refs_3_, ...), custom_call_target="tpu_custom_call", output_to_operand_aliasing={{}: (6, {})} | custom-call | tf_op jit(solution)/shard_map/pallas_call | solution.py:165
  95.3 2.8 %shard_map.63.refs_6_ = f32[3072,512]{1,0:T(8,128)} custom-call(bf16[896,512]{1,0:T(8,128)(2,1)S(1)} %add_convert_fusion.refs_0_, bf16[896,512]{1,0:T(8,128)(2,1)S(1)} %collective-permute-done.18.refs_1_, bf16[896,512]{1,0:T(8,128)(2,1)S(1)} %collective-permute-done.19.refs_2_, ...), custom_call_target="tpu_custom_call", output_to_operand_aliasing={{}: (6, {})} | custom-call | tf_op jit(solution)/shard_map/pallas_call | solution.py:165
  98.1 2.1 %shard_map.64.refs_3_ = f32[3072,512]{1,0:T(8,128)} custom-call(bf16[512,512]{1,0:T(8,128)(2,1)S(1)} %add_convert_fusion.2.refs_0_, bf16[512,512]{1,0:T(8,128)(2,1)S(1)} %collective-permute-done.15.refs_1_, bf16[512,512]{1,0:T(8,128)(2,1)S(1)} %collective-permute-done.16.refs_2_, ...), custom_call_target="tpu_custom_call", output_to_operand_aliasing={{}: (6, {})} | custom-call | tf_op jit(solution)/shard_map/pallas_call | solution.py:165
  100.2 1.2 %shard_map.65.refs_3_ = f32[3072,512]{1,0:T(8,128)} custom-call(bf16[288,512]{1,0:T(8,128)(2,1)S(1)} %collective-permute-done.13.refs_0_, bf16[2048,512]{1,0:T(8,128)(2,1)S(1)} %copy-done, f32[288,512]{1,0:T(8,128)S(1)} %shard_map.60.refs_2_, f32[3072,512]{1,0:T(8,128)} %shard_map.64.refs_3_), custom_call_target="tpu_custom_call", output_to_operand_aliasing={{}: (3, {})} | custom-call | tf_op jit(solution)/shard_map/pallas_call | solution.py:165
  101.4 1.0 shard_map.66.refs_6_
  102.4 1.1 %shard_map.67 = f32[3072,512]{1,0:T(8,128)} custom-call(bf16[128,512]{1,0:T(8,128)(2,1)S(1)} %collective-permute-done.4.refs_0_, bf16[64,512]{1,0:T(8,128)(2,1)S(1)} %collective-permute-done.5.refs_1_, bf16[64,512]{1,0:T(8,128)(2,1)S(1)} %collective-permute-done.6.refs_2_, bf16[2048,512]{1,0:T(8,128)(2,1)S(1)} %copy-done, ...), custom_call_target="tpu_custom_call", output_to_operand_aliasing={{}: (6, {})} | custom-call | tf_op jit(solution)/shard_map/pallas_call | solution.py:192
  (65 shorter events, 4.9 us)
Async XLA Ops:
  1.1 16.2 %copy-start.3 = (f32[512]{0:T(512)S(1)}, f32[512]{0:T(512)}, u32[]{:S(2)}) copy-start(f32[512]{0:T(512)} %param.6) | copy-start | bytes 6148
  1.1 16.2 %copy-start.2 = (f32[512]{0:T(512)S(1)}, f32[512]{0:T(512)}, u32[]{:S(2)}) copy-start(f32[512]{0:T(512)} %param.7) | copy-start | bytes 6148
  4.2 4.6 %collective-permute-start = (f32[2,512]{1,0:T(2,128)S(1)}, f32[2,512]{1,0:T(2,128)S(1)}, u32[]{:S(2)}, u32[]{:S(2)}) collective-permute-start(f32[2,512]{1,0:T(2,128)S(1)} %get-tuple-element.13), channel_id=1, source_target_pairs={{0,4},{4,0},{8,12},{12,8},{16,20},{20,16},{24,28},{28,24},{1,5},{5... | collective-permute-start | bytes 12296 | tf_op jit(solution)/shard_map/ppermute | solution.py:233
  8.8 3.8 %collective-permute-start.1 = (f32[2,512]{1,0:T(2,128)S(1)}, f32[2,512]{1,0:T(2,128)S(1)}, u32[]{:S(2)}, u32[]{:S(2)}) collective-permute-start(f32[2,512]{1,0:T(2,128)S(1)} %pad_maximum_fusion.1), channel_id=1, source_target_pairs={{0,8},{4,12},{8,0},{12,4},{16,24},{20,28},{24,16},{28,20},{1,9},{5... | collective-permute-start | bytes 12296 | tf_op jit(solution)/shard_map/ppermute | solution.py:233
  12.6 4.7 %collective-permute-start.2 = (f32[2,512]{1,0:T(2,128)S(1)}, f32[2,512]{1,0:T(2,128)S(1)}, u32[]{:S(2)}, u32[]{:S(2)}) collective-permute-start(f32[2,512]{1,0:T(2,128)S(1)} %pad_maximum_fusion.2), channel_id=1, source_target_pairs={{0,16},{4,20},{8,24},{12,28},{16,0},{20,4},{24,8},{28,12},{1,17},{... | collective-permute-start | bytes 12296 | tf_op jit(solution)/shard_map/ppermute | solution.py:233
  15.7 33.8 %collective-permute-start.26 = (bf16[256,512]{1,0:T(8,128)(2,1)S(1)}, bf16[256,512]{1,0:T(8,128)(2,1)S(1)}, u32[]{:S(2)}, u32[]{:S(2)}) collective-permute-start(bf16[256,512]{1,0:T(8,128)(2,1)S(1)} %get-tuple-element.16), channel_id=1, source_target_pairs={{0,2},{1,3},{2,0},{3,1},{4,6},{5,7},{6,4},{7,5},{8,10},{9,11},{10,... | collective-permute-start | bytes 786440 | tf_op jit(solution)/shard_map/ppermute | solution.py:213
  17.9 5.0 %collective-permute-start.23 = (f32[4,512]{1,0:T(4,128)S(1)}, f32[4,512]{1,0:T(4,128)S(1)}, u32[]{:S(2)}, u32[]{:S(2)}) collective-permute-start(f32[4,512]{1,0:T(4,128)S(1)} %pad_maximum_fusion), channel_id=1, source_target_pairs={{0,2},{1,3},{2,0},{3,1},{4,6},{5,7},{6,4},{7,5},{8,10},{9,11},{10,... | collective-permute-start | bytes 24584 | tf_op jit(solution)/shard_map/ppermute | solution.py:213
  19.8 5.7 %collective-permute-start.3 = (bf16[128,512]{1,0:T(8,128)(2,1)S(1)}, bf16[128,512]{1,0:T(8,128)(2,1)S(1)}, u32[]{:S(2)}, u32[]{:S(2)}) collective-permute-start(bf16[128,512]{1,0:T(8,128)(2,1)S(1)} %add_convert_fusion.7.refs_0_), channel_id=1, source_target_pairs={{0,2},{1,3},{2,0},{3,1},{4,6},{5,7},{6,4},{7,5},{8,10},{9,11},{10,... | collective-permute-start | bytes 393224 | tf_op jit(solution)/shard_map/ppermute | solution.py:213
  20.1 6.1 %collective-permute-start.7 = (bf16[128,512]{1,0:T(8,128)(2,1)S(1)}, bf16[128,512]{1,0:T(8,128)(2,1)S(1)}, u32[]{:S(2)}, u32[]{:S(2)}) collective-permute-start(bf16[128,512]{1,0:T(8,128)(2,1)S(1)} %add_convert_fusion.7.refs_0_), channel_id=1, source_target_pairs={{0,1},{1,0},{2,3},{3,2},{4,5},{5,4},{6,7},{7,6},{8,9},{9,8},{10,11... | collective-permute-start | bytes 393224 | tf_op jit(solution)/shard_map/ppermute | solution.py:219
  20.1 6.1 %collective-permute-start.11 = (bf16[160,512]{1,0:T(8,128)(2,1)S(1)}, bf16[160,512]{1,0:T(8,128)(2,1)S(1)}, u32[]{:S(2)}, u32[]{:S(2)}) collective-permute-start(bf16[160,512]{1,0:T(8,128)(2,1)S(1)} %add_convert_fusion.6.refs_0_), channel_id=1, source_target_pairs={{0,1},{1,0},{2,3},{3,2},{4,5},{5,4},{6,7},{7,6},{8,9},{9,8},{10,11... | collective-permute-start | bytes 491528 | tf_op jit(solution)/shard_map/ppermute | solution.py:219
  22.9 1.3 %collective-permute-start.8 = (bf16[64,512]{1,0:T(8,128)(2,1)S(1)}, bf16[64,512]{1,0:T(8,128)(2,1)S(1)}, u32[]{:S(2)}, u32[]{:S(2)}) collective-permute-start(bf16[64,512]{1,0:T(8,128)(2,1)S(1)} %add_convert_fusion.8.refs_0_), channel_id=1, source_target_pairs={{0,1},{1,0},{2,3},{3,2},{4,5},{5,4},{6,7},{7,6},{8,9},{9,8},{10,11... | collective-permute-start | bytes 196616 | tf_op jit(solution)/shard_map/ppermute | solution.py:219
  24.2 52.3 %collective-permute-start.22 = (bf16[768,512]{1,0:T(8,128)(2,1)S(1)}, bf16[768,512]{1,0:T(8,128)(2,1)S(1)}, u32[]{:S(2)}, u32[]{:S(2)}) collective-permute-start(bf16[768,512]{1,0:T(8,128)(2,1)S(1)} %get-tuple-element.14), channel_id=1, source_target_pairs={{0,2},{1,3},{2,0},{3,1},{4,6},{5,7},{6,4},{7,5},{8,10},{9,11},{10,... | collective-permute-start | bytes 2359304 | tf_op jit(solution)/shard_map/ppermute | solution.py:213
  25.5 22.6 %collective-permute-start.9 = (bf16[160,512]{1,0:T(8,128)(2,1)S(1)}, bf16[160,512]{1,0:T(8,128)(2,1)S(1)}, u32[]{:S(2)}, u32[]{:S(2)}) collective-permute-start(bf16[160,512]{1,0:T(8,128)(2,1)S(1)} %add_convert_fusion.6.refs_0_), channel_id=1, source_target_pairs={{0,2},{1,3},{2,0},{3,1},{4,6},{5,7},{6,4},{7,5},{8,10},{9,11},{10,... | collective-permute-start | bytes 491528 | tf_op jit(solution)/shard_map/ppermute | solution.py:213
  26.2 23.3 %collective-permute-start.25 = (bf16[256,512]{1,0:T(8,128)(2,1)S(1)}, bf16[256,512]{1,0:T(8,128)(2,1)S(1)}, u32[]{:S(2)}, u32[]{:S(2)}) collective-permute-start(bf16[256,512]{1,0:T(8,128)(2,1)S(1)} %add_convert_fusion.5.refs_0_), channel_id=1, source_target_pairs={{0,1},{1,0},{2,3},{3,2},{4,5},{5,4},{6,7},{7,6},{8,9},{9,8},{10,11... | collective-permute-start | bytes 786440 | tf_op jit(solution)/shard_map/ppermute | solution.py:219
  26.2 50.7 %collective-permute-start.19 = (bf16[896,512]{1,0:T(8,128)(2,1)S(1)}, bf16[896,512]{1,0:T(8,128)(2,1)S(1)}, u32[]{:S(2)}, u32[]{:S(2)}) collective-permute-start(bf16[896,512]{1,0:T(8,128)(2,1)S(1)} %add_convert_fusion.refs_0_), channel_id=1, source_target_pairs={{0,2},{1,3},{2,0},{3,1},{4,6},{5,7},{6,4},{7,5},{8,10},{9,11},{10,... | collective-permute-start | bytes 2752520 | tf_op jit(solution)/shard_map/ppermute | solution.py:213
  48.1 26.0 %collective-permute-start.12 = (bf16[288,512]{1,0:T(8,128)(2,1)S(1)}, bf16[288,512]{1,0:T(8,128)(2,1)S(1)}, u32[]{:S(2)}, u32[]{:S(2)}) collective-permute-start(bf16[288,512]{1,0:T(8,128)(2,1)S(1)} %add_convert_fusion.3.refs_0_), channel_id=1, source_target_pairs={{0,2},{1,3},{2,0},{3,1},{4,6},{5,7},{6,4},{7,5},{8,10},{9,11},{10,... | collective-permute-start | bytes 884744 | tf_op jit(solution)/shard_map/ppermute | solution.py:213
  49.5 24.6 %collective-permute-start.14 = (bf16[288,512]{1,0:T(8,128)(2,1)S(1)}, bf16[288,512]{1,0:T(8,128)(2,1)S(1)}, u32[]{:S(2)}, u32[]{:S(2)}) collective-permute-start(bf16[288,512]{1,0:T(8,128)(2,1)S(1)} %add_convert_fusion.3.refs_0_), channel_id=1, source_target_pairs={{0,1},{1,0},{2,3},{3,2},{4,5},{5,4},{6,7},{7,6},{8,9},{9,8},{10,11... | collective-permute-start | bytes 884744 | tf_op jit(solution)/shard_map/ppermute | solution.py:219
  49.5 35.0 %collective-permute-start.16 = (bf16[512,512]{1,0:T(8,128)(2,1)S(1)}, bf16[512,512]{1,0:T(8,128)(2,1)S(1)}, u32[]{:S(2)}, u32[]{:S(2)}) collective-permute-start(bf16[512,512]{1,0:T(8,128)(2,1)S(1)} %add_convert_fusion.2.refs_0_), channel_id=1, source_target_pairs={{0,2},{1,3},{2,0},{3,1},{4,6},{5,7},{6,4},{7,5},{8,10},{9,11},{10,... | collective-permute-start | bytes 1572872 | tf_op jit(solution)/shard_map/ppermute | solution.py:213
  50.3 39.1 %copy-start = (bf16[2048,512]{1,0:T(8,128)(2,1)S(1)}, bf16[2048,512]{1,0:T(8,128)(2,1)}, u32[]{:S(2)}) copy-start(bf16[2048,512]{1,0:T(8,128)(2,1)} %refs_3_.7) | copy-start | bytes 6291460
  50.3 39.1 %copy-start.1 = (f32[512]{0:T(512)S(1)}, f32[512]{0:T(512)}, u32[]{:S(2)}) copy-start(f32[512]{0:T(512)} %param.9) | copy-start | bytes 6148
  74.1 10.4 %collective-permute-start.15 = (bf16[512,512]{1,0:T(8,128)(2,1)S(1)}, bf16[512,512]{1,0:T(8,128)(2,1)S(1)}, u32[]{:S(2)}, u32[]{:S(2)}) collective-permute-start(bf16[512,512]{1,0:T(8,128)(2,1)S(1)} %add_convert_fusion.2.refs_0_), channel_id=1, source_target_pairs={{0,1},{1,0},{2,3},{3,2},{4,5},{5,4},{6,7},{7,6},{8,9},{9,8},{10,11... | collective-permute-start | bytes 1572872 | tf_op jit(solution)/shard_map/ppermute | solution.py:219
  74.1 2.3 %collective-permute-start.27 = (bf16[256,512]{1,0:T(8,128)(2,1)S(1)}, bf16[256,512]{1,0:T(8,128)(2,1)S(1)}, u32[]{:S(2)}, u32[]{:S(2)}) collective-permute-start(bf16[256,512]{1,0:T(8,128)(2,1)S(1)} %add_convert_fusion.4.refs_2_), channel_id=1, source_target_pairs={{0,1},{1,0},{2,3},{3,2},{4,5},{5,4},{6,7},{7,6},{8,9},{9,8},{10,11... | collective-permute-start | bytes 786440 | tf_op jit(solution)/shard_map/ppermute | solution.py:219
  76.4 8.7 %collective-permute-start.21 = (bf16[768,512]{1,0:T(8,128)(2,1)S(1)}, bf16[768,512]{1,0:T(8,128)(2,1)S(1)}, u32[]{:S(2)}, u32[]{:S(2)}) collective-permute-start(bf16[768,512]{1,0:T(8,128)(2,1)S(1)} %add_convert_fusion.1.refs_0_), channel_id=1, source_target_pairs={{0,1},{1,0},{2,3},{3,2},{4,5},{5,4},{6,7},{7,6},{8,9},{9,8},{10,11... | collective-permute-start | bytes 2359304 | tf_op jit(solution)/shard_map/ppermute | solution.py:219
  76.5 8.6 %collective-permute-start.18 = (bf16[896,512]{1,0:T(8,128)(2,1)S(1)}, bf16[896,512]{1,0:T(8,128)(2,1)S(1)}, u32[]{:S(2)}, u32[]{:S(2)}) collective-permute-start(bf16[896,512]{1,0:T(8,128)(2,1)S(1)} %add_convert_fusion.refs_0_), channel_id=1, source_target_pairs={{0,1},{1,0},{2,3},{3,2},{4,5},{5,4},{6,7},{7,6},{8,9},{9,8},{10,11... | collective-permute-start | bytes 2752520 | tf_op jit(solution)/shard_map/ppermute | solution.py:219
  76.9 12.2 %collective-permute-start.20 = (bf16[896,512]{1,0:T(8,128)(2,1)S(1)}, bf16[896,512]{1,0:T(8,128)(2,1)S(1)}, u32[]{:S(2)}, u32[]{:S(2)}) collective-permute-start(bf16[896,512]{1,0:T(8,128)(2,1)S(1)} %collective-permute-done.19.refs_2_), channel_id=1, source_target_pairs={{0,1},{1,0},{2,3},{3,2},{4,5},{5,4},{6,7},{7,6},{8,9},{9,8},{10,11... | collective-permute-start | bytes 2752520 | tf_op jit(solution)/shard_map/ppermute | solution.py:219
  84.5 3.2 %collective-permute-start.24 = (bf16[768,512]{1,0:T(8,128)(2,1)S(1)}, bf16[768,512]{1,0:T(8,128)(2,1)S(1)}, u32[]{:S(2)}, u32[]{:S(2)}) collective-permute-start(bf16[768,512]{1,0:T(8,128)(2,1)S(1)} %fusion.refs_2_), channel_id=1, source_target_pairs={{0,1},{1,0},{2,3},{3,2},{4,5},{5,4},{6,7},{7,6},{8,9},{9,8},{10,11... | collective-permute-start | bytes 2359304 | tf_op jit(solution)/shard_map/ppermute | solution.py:219
  84.5 3.0 %collective-permute-start.17 = (bf16[512,512]{1,0:T(8,128)(2,1)S(1)}, bf16[512,512]{1,0:T(8,128)(2,1)S(1)}, u32[]{:S(2)}, u32[]{:S(2)}) collective-permute-start(bf16[512,512]{1,0:T(8,128)(2,1)S(1)} %collective-permute-done.16.refs_2_), channel_id=1, source_target_pairs={{0,1},{1,0},{2,3},{3,2},{4,5},{5,4},{6,7},{7,6},{8,9},{9,8},{10,11... | collective-permute-start | bytes 1572872 | tf_op jit(solution)/shard_map/ppermute | solution.py:219
  85.0 15.2 %collective-permute-start.13 = (bf16[288,512]{1,0:T(8,128)(2,1)S(1)}, bf16[288,512]{1,0:T(8,128)(2,1)S(1)}, u32[]{:S(2)}, u32[]{:S(2)}) collective-permute-start(bf16[288,512]{1,0:T(8,128)(2,1)S(1)} %collective-permute-done.12.refs_2_), channel_id=1, source_target_pairs={{0,1},{1,0},{2,3},{3,2},{4,5},{5,4},{6,7},{7,6},{8,9},{9,8},{10,11... | collective-permute-start | bytes 884744 | tf_op jit(solution)/shard_map/ppermute | solution.py:219
  85.1 16.3 %collective-permute-start.10 = (bf16[160,512]{1,0:T(8,128)(2,1)S(1)}, bf16[160,512]{1,0:T(8,128)(2,1)S(1)}, u32[]{:S(2)}, u32[]{:S(2)}) collective-permute-start(bf16[160,512]{1,0:T(8,128)(2,1)S(1)} %collective-permute-done.9.refs_2_), channel_id=1, source_target_pairs={{0,1},{1,0},{2,3},{3,2},{4,5},{5,4},{6,7},{7,6},{8,9},{9,8},{10,11... | collective-permute-start | bytes 491528 | tf_op jit(solution)/shard_map/ppermute | solution.py:219
  87.5 14.9 %collective-permute-start.4 = (bf16[128,512]{1,0:T(8,128)(2,1)S(1)}, bf16[128,512]{1,0:T(8,128)(2,1)S(1)}, u32[]{:S(2)}, u32[]{:S(2)}) collective-permute-start(bf16[128,512]{1,0:T(8,128)(2,1)S(1)} %collective-permute-done.3.refs_2_), channel_id=1, source_target_pairs={{0,1},{1,0},{2,3},{3,2},{4,5},{5,4},{6,7},{7,6},{8,9},{9,8},{10,11... | collective-permute-start | bytes 393224 | tf_op jit(solution)/shard_map/ppermute | solution.py:219
  87.7 14.7 %collective-permute-start.5 = (bf16[64,512]{1,0:T(8,128)(2,1)S(1)}, bf16[64,512]{1,0:T(8,128)(2,1)S(1)}, u32[]{:S(2)}, u32[]{:S(2)}) collective-permute-start(bf16[64,512]{1,0:T(8,128)(2,1)S(1)} %add_convert_fusion.8.refs_0_), channel_id=1, source_target_pairs={{0,2},{1,3},{2,0},{3,1},{4,6},{5,7},{6,4},{7,5},{8,10},{9,11},{10,... | collective-permute-start | bytes 196616 | tf_op jit(solution)/shard_map/ppermute | solution.py:213
  89.0 13.4 %collective-permute-start.6 = (bf16[64,512]{1,0:T(8,128)(2,1)S(1)}, bf16[64,512]{1,0:T(8,128)(2,1)S(1)}, u32[]{:S(2)}, u32[]{:S(2)}) collective-permute-start(bf16[64,512]{1,0:T(8,128)(2,1)S(1)} %add_convert_fusion.8.refs_0_), channel_id=1, source_target_pairs={{0,3},{1,2},{2,1},{3,0},{4,7},{5,6},{6,5},{7,4},{8,11},{9,10},{10,... | collective-permute-start | bytes 196616 | tf_op jit(solution)/shard_map/ppermute | solution.py:216
where the time goes:
time: 104 us
  waiting for transfers between devices  61.7 us (59%)
  starting transfers between devices  22.1 us (21%)
  Pallas kernels  18.2 us (18%)
  other arithmetic  1.25 us (1%)
    ppermute x9, waiting for transfers between devices, to_far(): lax.ppermute(x, 'feat', [(i, (i + s) % feat) for i in range(feat)])  53.7 us
    pallas_call x6, Pallas kernels, layer(): pl.pallas_call(functools.partial(layer_kernel, places=places, first=first...  11.2 us
    ppermute x9, starting transfers between devices, to_far(): lax.ppermute(x, 'feat', [(i, (i + s) % feat) for i in range(feat)])  10.6 us
    ppermute x3, starting transfers between devices, local(): theirs = lax.ppermute(mine, 'dp', [(i, i ^ step) for i in range(dp)])  8.3 us
    ppermute x15, waiting for transfers between devices, to_near(): return lax.ppermute(x, 'feat', near)  4.75 us
    ppermute x3, waiting for transfers between devices, local(): theirs = lax.ppermute(mine, 'dp', [(i, i ^ step) for i in range(dp)])  3.24 us
    pallas_call x1, Pallas kernels, survey(): pl.pallas_call(functools.partial(survey_kernel, early=pieces, others=othe...  3 us
    ppermute x15, starting transfers between devices, to_near(): return lax.ppermute(x, 'feat', near)  2.83 us
  transfers between devices with their start and end apart: 28, of which 10 were waited for; matrix products, arithmetic and copies ran while one was open for 1% of the time, Pallas kernels for 12%

commit v1 on v0

--- a/solution.py
+++ b/solution.py
@@ -9,11 +9,12 @@
 
 
 UNITS = 96
-EARLY = (8, 24)
-LATE = (28, 16, 9, 5, 4)
+EARLY = (8, 20)
+LATE = (31, 17, 9, 5, 4)
 DIRECT = 2
-PIECE = 12
+PIECE = 10
 SPLIT = 3
+CROSSED = (5, 6)
 
 
 def grant(kib):
@@ -173,24 +174,24 @@
     )(*args)
 
 
-def finish_kernel(*refs, shifts):
+def finish_kernel(*refs, shifts, held):
     passed, far, cross = refs[:shifts], refs[shifts : 2 * shifts], refs[2 * shifts : 3 * shifts]
     w_ref, base_ref, tail_ref, _, out_ref, buf, sem = refs[3 * shifts :]
     count = buf.shape[0]
-    tail = product([x[...] for x in far], range(2, 2 + 2 * shifts, 2), w_ref, tail_ref[...])
+    tail = product([x[...] for x in far], range(held, held + 2 * shifts, 2), w_ref, tail_ref[...])
     xs = [jnp.concatenate([p[...], c[...]]) for p, c in zip(passed, cross)]
     base = jnp.concatenate([base_ref[...], tail])
-    buf[...] = jnp.maximum(product(xs, range(3, 3 + 2 * shifts, 2), w_ref, base), 0.0)
+    buf[...] = jnp.maximum(product(xs, range(5 - held, 5 - held + 2 * shifts, 2), w_ref, base), 0.0)
     copy = pltpu.make_async_copy(buf, out_ref.at[pl.ds(out_ref.shape[0] - count, count), :], sem)
     copy.start()
     copy.wait()
 
 
-def finish(passed, far, cross, weight, base, tail, out):
+def finish(passed, far, cross, held, weight, base, tail, out):
     count = base.shape[0] + tail.shape[0]
     vmem = 3 * len(passed) + 3
     return pl.pallas_call(
-        functools.partial(finish_kernel, shifts=len(passed)),
+        functools.partial(finish_kernel, shifts=len(passed), held=held),
         in_specs=[pl.BlockSpec(memory_space=pltpu.VMEM)] * vmem + [pl.BlockSpec(memory_space=pltpu.HBM)],
         out_specs=pl.BlockSpec(memory_space=pltpu.HBM),
         out_shape=jax.ShapeDtypeStruct(out.shape, out.dtype),
@@ -248,7 +249,7 @@
     last = len(EARLY) + len(LATE)
     for k in range(len(EARLY), last + 1):
         own[k] = normalize(k)
-        arrived[k] = to_far(own[k])
+        arrived[k] = (to_cross if k in CROSSED else to_far)(own[k])
     crossed = to_cross(own[last])
     offsets = (jnp.concatenate(found) - mean) * scale + beta
     table = to_far(jnp.concatenate([scale[None], offsets]))
@@ -271,16 +272,17 @@
     for k in range(last):
         xs = {0: own[k], 1: to_near(own[k])}
         for place, got in zip(places[2::2], arrived[k]):
-            xs[place], xs[place + 1] = got, to_near(got)
+            xs[place], xs[place + 1] = (to_near(got), got) if k in CROSSED else (got, to_near(got))
         wanted, base = places, bias
         if k >= last - SPLIT:
-            wanted = places[3::2]
+            wanted = places[2::2] if k in CROSSED else places[3::2]
             held = tuple(p for p in places if p not in wanted)
             base = part([xs[p] for p in held], held, weight, bias)
         xs = [xs[p] for p in wanted]
         if k < last - 1:
             out = layer(xs, wanted, weight, base, out, firsts[k] * unit, rows)
-    return finish(xs, arrived[last], crossed, weight, base, tail, out)
+    ends = (crossed, arrived[last], 3) if last - 1 in CROSSED else (arrived[last], crossed, 2)
+    return finish(xs, *ends, weight, base, tail, out)
 
 
 def solution(mesh):

time: 104 us -> 106 us (1.019)
  starting transfers between devices: 22.1 us -> 24.8 us
    ppermute x1 -> x3, waiting for transfers between devices: 0.01 us -> 36.4 us  [to_cross(): lax.ppermute(x, 'feat', [(i, (i + s) % feat ^ 1) for i in range(feat)])]
    ppermute x9 -> x7, waiting for transfers between devices: 53.7 us -> 19.2 us  [to_far(): lax.ppermute(x, 'feat', [(i, (i + s) % feat) for i in range(feat)])]
    ppermute x1 -> x3, starting transfers between devices: 0.36 us -> 4.29 us  [to_cross(): lax.ppermute(x, 'feat', [(i, (i + s) % feat ^ 1) for i in range(feat)])]
    ppermute x15, waiting for transfers between devices: 4.75 us -> 1.9 us  [to_near(): return lax.ppermute(x, 'feat', near)]
    ppermute x9 -> x7, starting transfers between devices: 10.6 us -> 7.73 us  [to_far(): lax.ppermute(x, 'feat', [(i, (i + s) % feat) for i in range(feat)])]
    ppermute x15, starting transfers between devices: 2.83 us -> 4.52 us  [to_near(): return lax.ppermute(x, 'feat', near)]
  transfers between devices with their start and end apart: 28 -> 28, of which waited for: 10 -> 9; matrix products, arithmetic and copies ran while one was open for 1% -> 1% of each run, Pallas kernels for 12% -> 12%
where the time goes in v1:
time: 106 us; the launch traced here: 105 us
  waiting for transfers between devices  60.7 us (57%)
  starting transfers between devices  24.8 us (23%)
  Pallas kernels  18.2 us (17%)
  other arithmetic  1.22 us (1%)
    ppermute x3, waiting for transfers between devices, to_cross(): lax.ppermute(x, 'feat', [(i, (i + s) % feat ^ 1) for i in range(feat)])  36.4 us
    ppermute x7, waiting for transfers between devices, to_far(): lax.ppermute(x, 'feat', [(i, (i + s) % feat) for i in range(feat)])  19.2 us
    pallas_call x6, Pallas kernels, layer(): pl.pallas_call(functools.partial(layer_kernel, places=places, first=first...  11.2 us
    ppermute x3, starting transfers between devices, local(): theirs = lax.ppermute(mine, 'dp', [(i, i ^ step) for i in range(dp)])  8.3 us
    ppermute x7, starting transfers between devices, to_far(): lax.ppermute(x, 'feat', [(i, (i + s) % feat) for i in range(feat)])  7.73 us
    ppermute x15, starting transfers between devices, to_near(): return lax.ppermute(x, 'feat', near)  4.52 us
    ppermute x3, starting transfers between devices, to_cross(): lax.ppermute(x, 'feat', [(i, (i + s) % feat ^ 1) for i in range(feat)])  4.29 us
    ppermute x3, waiting for transfers between devices, local(): theirs = lax.ppermute(mine, 'dp', [(i, i ^ step) for i in range(dp)])  3.24 us
  transfers between devices with their start and end apart: 28, of which 9 were waited for; matrix products, arithmetic and copies ran while one was open for 1% of the time, Pallas kernels for 12%

profile of v1, /device:TPU:0, one launch (start us, length us, event | category | flops | bytes accessed | tf_op | source)
XLA Modules:
  0.0 105.4 jit_solution(8816072686330184105)
XLA Ops:
  0.0 1.1 %shard_map.55 = (bf16[256,512]{1,0:T(8,128)(2,1)S(1)}, f32[1,512]{1,0:T(1,128)S(1)}) custom-call(f32[3072,512]{1,0:T(8,128)} %x_ref.3), custom_call_target="tpu_custom_call" | custom-call | tf_op jit(solution)/shard_map/pallas_call | solution.py:36
  1.2 3.0 %shard_map.56 = (f32[3072,512]{1,0:T(8,128)S(1)}, bf16[640,512]{1,0:T(8,128)(2,1)S(1)}, f32[2,512]{1,0:T(2,128)S(1)}, f32[2,512]{1,0:T(2,128)S(1)}) custom-call(f32[3072,512]{1,0:T(8,128)} %x_ref.3, f32[1,512]{1,0:T(1,128)S(1)} %get-tuple-element.11.pivot_ref), custom_call_target="tpu_custom_call" | custom-call | tf_op jit(solution)/shard_map/pallas_call | solution.py:88
  4.2 3.0 %collective-permute-start = (f32[2,512]{1,0:T(2,128)S(1)}, f32[2,512]{1,0:T(2,128)S(1)}, u32[]{:S(2)}, u32[]{:S(2)}) collective-permute-start(f32[2,512]{1,0:T(2,128)S(1)} %get-tuple-element.13), channel_id=1, source_target_pairs={{0,4},{4,0},{8,12},{12,8},{16,20},{20,16},{24,28},{28,24},{1,5},{5... | collective-permute-start | bytes 12296 | tf_op jit(solution)/shard_map/ppermute | solution.py:234
  7.2 1.6 %collective-permute-done = f32[2,512]{1,0:T(2,128)S(1)} collective-permute-done((f32[2,512]{1,0:T(2,128)S(1)}, f32[2,512]{1,0:T(2,128)S(1)}, u32[]{:S(2)}, u32[]{:S(2)}) %collective-permute-start) | collective-permute-done | bytes 4128 | tf_op jit(solution)/shard_map/ppermute | solution.py:234
  8.8 2.2 %collective-permute-start.1 = (f32[2,512]{1,0:T(2,128)S(1)}, f32[2,512]{1,0:T(2,128)S(1)}, u32[]{:S(2)}, u32[]{:S(2)}) collective-permute-start(f32[2,512]{1,0:T(2,128)S(1)} %pad_maximum_fusion.1), channel_id=1, source_target_pairs={{0,8},{4,12},{8,0},{12,4},{16,24},{20,28},{24,16},{28,20},{1,9},{5... | collective-permute-start | bytes 12296 | tf_op jit(solution)/shard_map/ppermute | solution.py:234
  11.0 1.6 %collective-permute-done.1 = f32[2,512]{1,0:T(2,128)S(1)} collective-permute-done((f32[2,512]{1,0:T(2,128)S(1)}, f32[2,512]{1,0:T(2,128)S(1)}, u32[]{:S(2)}, u32[]{:S(2)}) %collective-permute-start.1) | collective-permute-done | bytes 4128 | tf_op jit(solution)/shard_map/ppermute | solution.py:234
  12.6 3.1 %collective-permute-start.2 = (f32[2,512]{1,0:T(2,128)S(1)}, f32[2,512]{1,0:T(2,128)S(1)}, u32[]{:S(2)}, u32[]{:S(2)}) collective-permute-start(f32[2,512]{1,0:T(2,128)S(1)} %pad_maximum_fusion.2), channel_id=1, source_target_pairs={{0,16},{4,20},{8,24},{12,28},{16,0},{20,4},{24,8},{28,12},{1,17},{... | collective-permute-start | bytes 12296 | tf_op jit(solution)/shard_map/ppermute | solution.py:234
  15.7 1.5 %collective-permute-start.26 = (bf16[256,512]{1,0:T(8,128)(2,1)S(1)}, bf16[256,512]{1,0:T(8,128)(2,1)S(1)}, u32[]{:S(2)}, u32[]{:S(2)}) collective-permute-start(bf16[256,512]{1,0:T(8,128)(2,1)S(1)} %get-tuple-element.16), channel_id=1, source_target_pairs={{0,2},{1,3},{2,0},{3,1},{4,6},{5,7},{6,4},{7,5},{8,10},{9,11},{10,... | collective-permute-start | bytes 786440 | tf_op jit(solution)/shard_map/ppermute | solution.py:214
  17.9 1.9 %collective-permute-start.23 = (f32[4,512]{1,0:T(4,128)S(1)}, f32[4,512]{1,0:T(4,128)S(1)}, u32[]{:S(2)}, u32[]{:S(2)}) collective-permute-start(f32[4,512]{1,0:T(4,128)S(1)} %pad_maximum_fusion), channel_id=1, source_target_pairs={{0,2},{1,3},{2,0},{3,1},{4,6},{5,7},{6,4},{7,5},{8,10},{9,11},{10,... | collective-permute-start | bytes 24584 | tf_op jit(solution)/shard_map/ppermute | solution.py:214
  20.0 2.0 %collective-permute-start.3 = (bf16[128,512]{1,0:T(8,128)(2,1)S(1)}, bf16[128,512]{1,0:T(8,128)(2,1)S(1)}, u32[]{:S(2)}, u32[]{:S(2)}) collective-permute-start(bf16[128,512]{1,0:T(8,128)(2,1)S(1)} %add_convert_fusion.7.refs_0_), channel_id=1, source_target_pairs={{0,3},{1,2},{2,1},{3,0},{4,7},{5,6},{6,5},{7,4},{8,11},{9,10},{10,... | collective-permute-start | bytes 393224 | tf_op jit(solution)/shard_map/ppermute | solution.py:217
  22.0 3.0 %collective-permute-done.23 = f32[4,512]{1,0:T(4,128)S(1)} collective-permute-done((f32[4,512]{1,0:T(4,128)S(1)}, f32[4,512]{1,0:T(4,128)S(1)}, u32[]{:S(2)}, u32[]{:S(2)}) %collective-permute-start.23) | collective-permute-done | bytes 8224 | tf_op jit(solution)/shard_map/ppermute | solution.py:214
  25.6 19.4 %collective-permute-done.3.refs_2_ = bf16[128,512]{1,0:T(8,128)(2,1)S(1)} collective-permute-done((bf16[128,512]{1,0:T(8,128)(2,1)S(1)}, bf16[128,512]{1,0:T(8,128)(2,1)S(1)}, u32[]{:S(2)}, u32[]{:S(2)}) %collective-permute-start.3) | collective-permute-done | bytes 131104 | tf_op jit(solution)/shard_map/ppermute | solution.py:217
  45.0 0.9 collective-permute-start.11
  45.8 1.5 %collective-permute-start.22 = (bf16[640,512]{1,0:T(8,128)(2,1)S(1)}, bf16[640,512]{1,0:T(8,128)(2,1)S(1)}, u32[]{:S(2)}, u32[]{:S(2)}) collective-permute-start(bf16[640,512]{1,0:T(8,128)(2,1)S(1)} %get-tuple-element.14), channel_id=1, source_target_pairs={{0,2},{1,3},{2,0},{3,1},{4,6},{5,7},{6,4},{7,5},{8,10},{9,11},{10,... | collective-permute-start | bytes 1966088 | tf_op jit(solution)/shard_map/ppermute | solution.py:214
  47.3 0.9 collective-permute-start.9
  48.3 0.6 collective-permute-start.12
  48.9 17.0 %collective-permute-done.9.refs_2_ = bf16[160,512]{1,0:T(8,128)(2,1)S(1)} collective-permute-done((bf16[160,512]{1,0:T(8,128)(2,1)S(1)}, bf16[160,512]{1,0:T(8,128)(2,1)S(1)}, u32[]{:S(2)}, u32[]{:S(2)}) %collective-permute-start.9) | collective-permute-done | bytes 163872 | tf_op jit(solution)/shard_map/ppermute | solution.py:217
  66.0 0.9 collective-permute-start.14
  67.0 5.4 %collective-permute-done.12.refs_2_ = bf16[288,512]{1,0:T(8,128)(2,1)S(1)} collective-permute-done((bf16[288,512]{1,0:T(8,128)(2,1)S(1)}, bf16[288,512]{1,0:T(8,128)(2,1)S(1)}, u32[]{:S(2)}, u32[]{:S(2)}) %collective-permute-start.12) | collective-permute-done | bytes 294944 | tf_op jit(solution)/shard_map/ppermute | solution.py:214
  72.4 1.4 %collective-permute-start.16 = (bf16[544,512]{1,0:T(8,128)(2,1)S(1)}, bf16[544,512]{1,0:T(8,128)(2,1)S(1)}, u32[]{:S(2)}, u32[]{:S(2)}) collective-permute-start(bf16[544,512]{1,0:T(8,128)(2,1)S(1)} %add_convert_fusion.2.refs_0_), channel_id=1, source_target_pairs={{0,2},{1,3},{2,0},{3,1},{4,6},{5,7},{6,4},{7,5},{8,10},{9,11},{10,... | collective-permute-start | bytes 1671176 | tf_op jit(solution)/shard_map/ppermute | solution.py:214
  75.3 10.8 %collective-permute-done.16.refs_2_ = bf16[544,512]{1,0:T(8,128)(2,1)S(1)} collective-permute-done((bf16[544,512]{1,0:T(8,128)(2,1)S(1)}, bf16[544,512]{1,0:T(8,128)(2,1)S(1)}, u32[]{:S(2)}, u32[]{:S(2)}) %collective-permute-start.16) | collective-permute-done | bytes 557088 | tf_op jit(solution)/shard_map/ppermute | solution.py:214
  87.1 1.9 %collective-permute-done.17.refs_3_ = bf16[544,512]{1,0:T(8,128)(2,1)S(1)} collective-permute-done((bf16[544,512]{1,0:T(8,128)(2,1)S(1)}, bf16[544,512]{1,0:T(8,128)(2,1)S(1)}, u32[]{:S(2)}, u32[]{:S(2)}) %collective-permute-start.17) | collective-permute-done | bytes 557088 | tf_op jit(solution)/shard_map/ppermute | solution.py:220
  89.1 1.4 %collective-permute-start.5 = (bf16[64,512]{1,0:T(8,128)(2,1)S(1)}, bf16[64,512]{1,0:T(8,128)(2,1)S(1)}, u32[]{:S(2)}, u32[]{:S(2)}) collective-permute-start(bf16[64,512]{1,0:T(8,128)(2,1)S(1)} %add_convert_fusion.8.refs_0_), channel_id=1, source_target_pairs={{0,3},{1,2},{2,1},{3,0},{4,7},{5,6},{6,5},{7,4},{8,11},{9,10},{10,... | collective-permute-start | bytes 196616 | tf_op jit(solution)/shard_map/ppermute | solution.py:217
  90.5 0.6 collective-permute-start.6
  92.3 0.6 shard_map.60.refs_2_
  92.9 1.5 %shard_map.61.refs_6_ = f32[3072,512]{1,0:T(8,128)} custom-call(bf16[256,512]{1,0:T(8,128)(2,1)S(1)} %add_convert_fusion.5.refs_0_, bf16[256,512]{1,0:T(8,128)(2,1)S(1)} %collective-permute-done.25.refs_1_, bf16[256,512]{1,0:T(8,128)(2,1)S(1)} %add_convert_fusion.4.refs_2_, bf16[256,512]{1,0:T(8,128)(2,1)S(1)} %collective-permute-done.27.refs_3_, ...), custom_call_target="tpu_custom_call" | custom-call | tf_op jit(solution)/shard_map/pallas_call | solution.py:166
  94.4 2.3 %shard_map.62.refs_6_ = f32[3072,512]{1,0:T(8,128)} custom-call(bf16[640,512]{1,0:T(8,128)(2,1)S(1)} %add_convert_fusion.1.refs_0_, bf16[640,512]{1,0:T(8,128)(2,1)S(1)} %collective-permute-done.21.refs_1_, bf16[640,512]{1,0:T(8,128)(2,1)S(1)} %fusion.refs_2_, bf16[640,512]{1,0:T(8,128)(2,1)S(1)} %collective-permute-done.24.refs_3_, ...), custom_call_target="tpu_custom_call", output_to_operand_aliasing={{}: (6, {})} | custom-call | tf_op jit(solution)/shard_map/pallas_call | solution.py:166
  96.7 3.1 %shard_map.63.refs_6_ = f32[3072,512]{1,0:T(8,128)} custom-call(bf16[992,512]{1,0:T(8,128)(2,1)S(1)} %add_convert_fusion.refs_0_, bf16[992,512]{1,0:T(8,128)(2,1)S(1)} %collective-permute-done.18.refs_1_, bf16[992,512]{1,0:T(8,128)(2,1)S(1)} %collective-permute-done.19.refs_2_, ...), custom_call_target="tpu_custom_call", output_to_operand_aliasing={{}: (6, {})} | custom-call | tf_op jit(solution)/shard_map/pallas_call | solution.py:166
  99.8 2.2 %shard_map.64.refs_3_ = f32[3072,512]{1,0:T(8,128)} custom-call(bf16[544,512]{1,0:T(8,128)(2,1)S(1)} %add_convert_fusion.2.refs_0_, bf16[544,512]{1,0:T(8,128)(2,1)S(1)} %collective-permute-done.15.refs_1_, bf16[544,512]{1,0:T(8,128)(2,1)S(1)} %collective-permute-done.16.refs_2_, ...), custom_call_target="tpu_custom_call", output_to_operand_aliasing={{}: (6, {})} | custom-call | tf_op jit(solution)/shard_map/pallas_call | solution.py:166
  102.0 1.2 %shard_map.65.refs_3_ = f32[3072,512]{1,0:T(8,128)} custom-call(bf16[288,512]{1,0:T(8,128)(2,1)S(1)} %collective-permute-done.13.refs_0_, bf16[2048,512]{1,0:T(8,128)(2,1)S(1)} %copy-done, f32[288,512]{1,0:T(8,128)S(1)} %shard_map.60.refs_2_, f32[3072,512]{1,0:T(8,128)} %shard_map.64.refs_3_), custom_call_target="tpu_custom_call", output_to_operand_aliasing={{}: (3, {})} | custom-call | tf_op jit(solution)/shard_map/pallas_call | solution.py:166
  103.2 1.0 shard_map.66.refs_6_
  104.2 1.1 %shard_map.67 = f32[3072,512]{1,0:T(8,128)} custom-call(bf16[128,512]{1,0:T(8,128)(2,1)S(1)} %collective-permute-done.4.refs_0_, bf16[64,512]{1,0:T(8,128)(2,1)S(1)} %collective-permute-done.5.refs_1_, bf16[64,512]{1,0:T(8,128)(2,1)S(1)} %collective-permute-done.6.refs_2_, bf16[2048,512]{1,0:T(8,128)(2,1)S(1)} %copy-done, ...), custom_call_target="tpu_custom_call", output_to_operand_aliasing={{}: (6, {})} | custom-call | tf_op jit(solution)/shard_map/pallas_call | solution.py:193
  (65 shorter events, 5.4 us)
Async XLA Ops:
  1.1 16.2 %copy-start.3 = (f32[512]{0:T(512)S(1)}, f32[512]{0:T(512)}, u32[]{:S(2)}) copy-start(f32[512]{0:T(512)} %param.6) | copy-start | bytes 6148
  1.1 16.2 %copy-start.2 = (f32[512]{0:T(512)S(1)}, f32[512]{0:T(512)}, u32[]{:S(2)}) copy-start(f32[512]{0:T(512)} %param.7) | copy-start | bytes 6148
  4.2 4.6 %collective-permute-start = (f32[2,512]{1,0:T(2,128)S(1)}, f32[2,512]{1,0:T(2,128)S(1)}, u32[]{:S(2)}, u32[]{:S(2)}) collective-permute-start(f32[2,512]{1,0:T(2,128)S(1)} %get-tuple-element.13), channel_id=1, source_target_pairs={{0,4},{4,0},{8,12},{12,8},{16,20},{20,16},{24,28},{28,24},{1,5},{5... | collective-permute-start | bytes 12296 | tf_op jit(solution)/shard_map/ppermute | solution.py:234
  8.8 3.8 %collective-permute-start.1 = (f32[2,512]{1,0:T(2,128)S(1)}, f32[2,512]{1,0:T(2,128)S(1)}, u32[]{:S(2)}, u32[]{:S(2)}) collective-permute-start(f32[2,512]{1,0:T(2,128)S(1)} %pad_maximum_fusion.1), channel_id=1, source_target_pairs={{0,8},{4,12},{8,0},{12,4},{16,24},{20,28},{24,16},{28,20},{1,9},{5... | collective-permute-start | bytes 12296 | tf_op jit(solution)/shard_map/ppermute | solution.py:234
  12.6 4.7 %collective-permute-start.2 = (f32[2,512]{1,0:T(2,128)S(1)}, f32[2,512]{1,0:T(2,128)S(1)}, u32[]{:S(2)}, u32[]{:S(2)}) collective-permute-start(f32[2,512]{1,0:T(2,128)S(1)} %pad_maximum_fusion.2), channel_id=1, source_target_pairs={{0,16},{4,20},{8,24},{12,28},{16,0},{20,4},{24,8},{28,12},{1,17},{... | collective-permute-start | bytes 12296 | tf_op jit(solution)/shard_map/ppermute | solution.py:234
  15.7 32.6 %collective-permute-start.26 = (bf16[256,512]{1,0:T(8,128)(2,1)S(1)}, bf16[256,512]{1,0:T(8,128)(2,1)S(1)}, u32[]{:S(2)}, u32[]{:S(2)}) collective-permute-start(bf16[256,512]{1,0:T(8,128)(2,1)S(1)} %get-tuple-element.16), channel_id=1, source_target_pairs={{0,2},{1,3},{2,0},{3,1},{4,6},{5,7},{6,4},{7,5},{8,10},{9,11},{10,... | collective-permute-start | bytes 786440 | tf_op jit(solution)/shard_map/ppermute | solution.py:214
  17.9 7.1 %collective-permute-start.23 = (f32[4,512]{1,0:T(4,128)S(1)}, f32[4,512]{1,0:T(4,128)S(1)}, u32[]{:S(2)}, u32[]{:S(2)}) collective-permute-start(f32[4,512]{1,0:T(4,128)S(1)} %pad_maximum_fusion), channel_id=1, source_target_pairs={{0,2},{1,3},{2,0},{3,1},{4,6},{5,7},{6,4},{7,5},{8,10},{9,11},{10,... | collective-permute-start | bytes 24584 | tf_op jit(solution)/shard_map/ppermute | solution.py:214
  19.8 54.5 %collective-permute-start.19 = (bf16[992,512]{1,0:T(8,128)(2,1)S(1)}, bf16[992,512]{1,0:T(8,128)(2,1)S(1)}, u32[]{:S(2)}, u32[]{:S(2)}) collective-permute-start(bf16[992,512]{1,0:T(8,128)(2,1)S(1)} %add_convert_fusion.refs_0_), channel_id=1, source_target_pairs={{0,2},{1,3},{2,0},{3,1},{4,6},{5,7},{6,4},{7,5},{8,10},{9,11},{10,... | collective-permute-start | bytes 3047432 | tf_op jit(solution)/shard_map/ppermute | solution.py:214
  20.0 5.0 %collective-permute-start.8 = (bf16[64,512]{1,0:T(8,128)(2,1)S(1)}, bf16[64,512]{1,0:T(8,128)(2,1)S(1)}, u32[]{:S(2)}, u32[]{:S(2)}) collective-permute-start(bf16[64,512]{1,0:T(8,128)(2,1)S(1)} %add_convert_fusion.8.refs_0_), channel_id=1, source_target_pairs={{0,1},{1,0},{2,3},{3,2},{4,5},{5,4},{6,7},{7,6},{8,9},{9,8},{10,11... | collective-permute-start | bytes 196616 | tf_op jit(solution)/shard_map/ppermute | solution.py:220
  20.0 24.9 %collective-permute-start.3 = (bf16[128,512]{1,0:T(8,128)(2,1)S(1)}, bf16[128,512]{1,0:T(8,128)(2,1)S(1)}, u32[]{:S(2)}, u32[]{:S(2)}) collective-permute-start(bf16[128,512]{1,0:T(8,128)(2,1)S(1)} %add_convert_fusion.7.refs_0_), channel_id=1, source_target_pairs={{0,3},{1,2},{2,1},{3,0},{4,7},{5,6},{6,5},{7,4},{8,11},{9,10},{10,... | collective-permute-start | bytes 393224 | tf_op jit(solution)/shard_map/ppermute | solution.py:217
  25.1 20.8 %collective-permute-start.7 = (bf16[128,512]{1,0:T(8,128)(2,1)S(1)}, bf16[128,512]{1,0:T(8,128)(2,1)S(1)}, u32[]{:S(2)}, u32[]{:S(2)}) collective-permute-start(bf16[128,512]{1,0:T(8,128)(2,1)S(1)} %add_convert_fusion.7.refs_0_), channel_id=1, source_target_pairs={{0,1},{1,0},{2,3},{3,2},{4,5},{5,4},{6,7},{7,6},{8,9},{9,8},{10,11... | collective-permute-start | bytes 393224 | tf_op jit(solution)/shard_map/ppermute | solution.py:220
  25.1 41.8 %collective-permute-start.25 = (bf16[256,512]{1,0:T(8,128)(2,1)S(1)}, bf16[256,512]{1,0:T(8,128)(2,1)S(1)}, u32[]{:S(2)}, u32[]{:S(2)}) collective-permute-start(bf16[256,512]{1,0:T(8,128)(2,1)S(1)} %add_convert_fusion.5.refs_0_), channel_id=1, source_target_pairs={{0,1},{1,0},{2,3},{3,2},{4,5},{5,4},{6,7},{7,6},{8,9},{9,8},{10,11... | collective-permute-start | bytes 786440 | tf_op jit(solution)/shard_map/ppermute | solution.py:220
  45.0 2.4 %collective-permute-start.11 = (bf16[160,512]{1,0:T(8,128)(2,1)S(1)}, bf16[160,512]{1,0:T(8,128)(2,1)S(1)}, u32[]{:S(2)}, u32[]{:S(2)}) collective-permute-start(bf16[160,512]{1,0:T(8,128)(2,1)S(1)} %add_convert_fusion.6.refs_0_), channel_id=1, source_target_pairs={{0,1},{1,0},{2,3},{3,2},{4,5},{5,4},{6,7},{7,6},{8,9},{9,8},{10,11... | collective-permute-start | bytes 491528 | tf_op jit(solution)/shard_map/ppermute | solution.py:220
  45.8 28.8 %collective-permute-start.22 = (bf16[640,512]{1,0:T(8,128)(2,1)S(1)}, bf16[640,512]{1,0:T(8,128)(2,1)S(1)}, u32[]{:S(2)}, u32[]{:S(2)}) collective-permute-start(bf16[640,512]{1,0:T(8,128)(2,1)S(1)} %get-tuple-element.14), channel_id=1, source_target_pairs={{0,2},{1,3},{2,0},{3,1},{4,6},{5,7},{6,4},{7,5},{8,10},{9,11},{10,... | collective-permute-start | bytes 1966088 | tf_op jit(solution)/shard_map/ppermute | solution.py:214
  47.3 18.6 %collective-permute-start.9 = (bf16[160,512]{1,0:T(8,128)(2,1)S(1)}, bf16[160,512]{1,0:T(8,128)(2,1)S(1)}, u32[]{:S(2)}, u32[]{:S(2)}) collective-permute-start(bf16[160,512]{1,0:T(8,128)(2,1)S(1)} %add_convert_fusion.6.refs_0_), channel_id=1, source_target_pairs={{0,3},{1,2},{2,1},{3,0},{4,7},{5,6},{6,5},{7,4},{8,11},{9,10},{10,... | collective-permute-start | bytes 491528 | tf_op jit(solution)/shard_map/ppermute | solution.py:217
  48.3 24.1 %collective-permute-start.12 = (bf16[288,512]{1,0:T(8,128)(2,1)S(1)}, bf16[288,512]{1,0:T(8,128)(2,1)S(1)}, u32[]{:S(2)}, u32[]{:S(2)}) collective-permute-start(bf16[288,512]{1,0:T(8,128)(2,1)S(1)} %add_convert_fusion.3.refs_0_), channel_id=1, source_target_pairs={{0,2},{1,3},{2,0},{3,1},{4,6},{5,7},{6,4},{7,5},{8,10},{9,11},{10,... | collective-permute-start | bytes 884744 | tf_op jit(solution)/shard_map/ppermute | solution.py:214
  66.0 7.8 %collective-permute-start.14 = (bf16[288,512]{1,0:T(8,128)(2,1)S(1)}, bf16[288,512]{1,0:T(8,128)(2,1)S(1)}, u32[]{:S(2)}, u32[]{:S(2)}) collective-permute-start(bf16[288,512]{1,0:T(8,128)(2,1)S(1)} %add_convert_fusion.3.refs_0_), channel_id=1, source_target_pairs={{0,1},{1,0},{2,3},{3,2},{4,5},{5,4},{6,7},{7,6},{8,9},{9,8},{10,11... | collective-permute-start | bytes 884744 | tf_op jit(solution)/shard_map/ppermute | solution.py:220
  66.8 7.0 %collective-permute-start.27 = (bf16[256,512]{1,0:T(8,128)(2,1)S(1)}, bf16[256,512]{1,0:T(8,128)(2,1)S(1)}, u32[]{:S(2)}, u32[]{:S(2)}) collective-permute-start(bf16[256,512]{1,0:T(8,128)(2,1)S(1)} %add_convert_fusion.4.refs_2_), channel_id=1, source_target_pairs={{0,1},{1,0},{2,3},{3,2},{4,5},{5,4},{6,7},{7,6},{8,9},{9,8},{10,11... | collective-permute-start | bytes 786440 | tf_op jit(solution)/shard_map/ppermute | solution.py:220
  67.0 24.1 %copy-start = (bf16[2048,512]{1,0:T(8,128)(2,1)S(1)}, bf16[2048,512]{1,0:T(8,128)(2,1)}, u32[]{:S(2)}) copy-start(bf16[2048,512]{1,0:T(8,128)(2,1)} %refs_3_.7) | copy-start | bytes 6291460
  67.0 24.1 %copy-start.1 = (f32[512]{0:T(512)S(1)}, f32[512]{0:T(512)}, u32[]{:S(2)}) copy-start(f32[512]{0:T(512)} %param.9) | copy-start | bytes 6148
  72.4 13.7 %collective-permute-start.16 = (bf16[544,512]{1,0:T(8,128)(2,1)S(1)}, bf16[544,512]{1,0:T(8,128)(2,1)S(1)}, u32[]{:S(2)}, u32[]{:S(2)}) collective-permute-start(bf16[544,512]{1,0:T(8,128)(2,1)S(1)} %add_convert_fusion.2.refs_0_), channel_id=1, source_target_pairs={{0,2},{1,3},{2,0},{3,1},{4,6},{5,7},{6,4},{7,5},{8,10},{9,11},{10,... | collective-permute-start | bytes 1671176 | tf_op jit(solution)/shard_map/ppermute | solution.py:214
  73.8 12.3 %collective-permute-start.15 = (bf16[544,512]{1,0:T(8,128)(2,1)S(1)}, bf16[544,512]{1,0:T(8,128)(2,1)S(1)}, u32[]{:S(2)}, u32[]{:S(2)}) collective-permute-start(bf16[544,512]{1,0:T(8,128)(2,1)S(1)} %add_convert_fusion.2.refs_0_), channel_id=1, source_target_pairs={{0,1},{1,0},{2,3},{3,2},{4,5},{5,4},{6,7},{7,6},{8,9},{9,8},{10,11... | collective-permute-start | bytes 1671176 | tf_op jit(solution)/shard_map/ppermute | solution.py:220
  73.8 12.8 %collective-permute-start.18 = (bf16[992,512]{1,0:T(8,128)(2,1)S(1)}, bf16[992,512]{1,0:T(8,128)(2,1)S(1)}, u32[]{:S(2)}, u32[]{:S(2)}) collective-permute-start(bf16[992,512]{1,0:T(8,128)(2,1)S(1)} %add_convert_fusion.refs_0_), channel_id=1, source_target_pairs={{0,1},{1,0},{2,3},{3,2},{4,5},{5,4},{6,7},{7,6},{8,9},{9,8},{10,11... | collective-permute-start | bytes 3047432 | tf_op jit(solution)/shard_map/ppermute | solution.py:220
  74.3 16.2 %collective-permute-start.20 = (bf16[992,512]{1,0:T(8,128)(2,1)S(1)}, bf16[992,512]{1,0:T(8,128)(2,1)S(1)}, u32[]{:S(2)}, u32[]{:S(2)}) collective-permute-start(bf16[992,512]{1,0:T(8,128)(2,1)S(1)} %collective-permute-done.19.refs_2_), channel_id=1, source_target_pairs={{0,1},{1,0},{2,3},{3,2},{4,5},{5,4},{6,7},{7,6},{8,9},{9,8},{10,11... | collective-permute-start | bytes 3047432 | tf_op jit(solution)/shard_map/ppermute | solution.py:220
  74.6 12.0 %collective-permute-start.21 = (bf16[640,512]{1,0:T(8,128)(2,1)S(1)}, bf16[640,512]{1,0:T(8,128)(2,1)S(1)}, u32[]{:S(2)}, u32[]{:S(2)}) collective-permute-start(bf16[640,512]{1,0:T(8,128)(2,1)S(1)} %add_convert_fusion.1.refs_0_), channel_id=1, source_target_pairs={{0,1},{1,0},{2,3},{3,2},{4,5},{5,4},{6,7},{7,6},{8,9},{9,8},{10,11... | collective-permute-start | bytes 1966088 | tf_op jit(solution)/shard_map/ppermute | solution.py:220
  86.1 3.0 %collective-permute-start.24 = (bf16[640,512]{1,0:T(8,128)(2,1)S(1)}, bf16[640,512]{1,0:T(8,128)(2,1)S(1)}, u32[]{:S(2)}, u32[]{:S(2)}) collective-permute-start(bf16[640,512]{1,0:T(8,128)(2,1)S(1)} %fusion.refs_2_), channel_id=1, source_target_pairs={{0,1},{1,0},{2,3},{3,2},{4,5},{5,4},{6,7},{7,6},{8,9},{9,8},{10,11... | collective-permute-start | bytes 1966088 | tf_op jit(solution)/shard_map/ppermute | solution.py:220
  86.1 2.9 %collective-permute-start.17 = (bf16[544,512]{1,0:T(8,128)(2,1)S(1)}, bf16[544,512]{1,0:T(8,128)(2,1)S(1)}, u32[]{:S(2)}, u32[]{:S(2)}) collective-permute-start(bf16[544,512]{1,0:T(8,128)(2,1)S(1)} %collective-permute-done.16.refs_2_), channel_id=1, source_target_pairs={{0,1},{1,0},{2,3},{3,2},{4,5},{5,4},{6,7},{7,6},{8,9},{9,8},{10,11... | collective-permute-start | bytes 1671176 | tf_op jit(solution)/shard_map/ppermute | solution.py:220
  86.6 15.4 %collective-permute-start.13 = (bf16[288,512]{1,0:T(8,128)(2,1)S(1)}, bf16[288,512]{1,0:T(8,128)(2,1)S(1)}, u32[]{:S(2)}, u32[]{:S(2)}) collective-permute-start(bf16[288,512]{1,0:T(8,128)(2,1)S(1)} %collective-permute-done.12.refs_2_), channel_id=1, source_target_pairs={{0,1},{1,0},{2,3},{3,2},{4,5},{5,4},{6,7},{7,6},{8,9},{9,8},{10,11... | collective-permute-start | bytes 884744 | tf_op jit(solution)/shard_map/ppermute | solution.py:220
  86.7 16.5 %collective-permute-start.10 = (bf16[160,512]{1,0:T(8,128)(2,1)S(1)}, bf16[160,512]{1,0:T(8,128)(2,1)S(1)}, u32[]{:S(2)}, u32[]{:S(2)}) collective-permute-start(bf16[160,512]{1,0:T(8,128)(2,1)S(1)} %collective-permute-done.9.refs_2_), channel_id=1, source_target_pairs={{0,1},{1,0},{2,3},{3,2},{4,5},{5,4},{6,7},{7,6},{8,9},{9,8},{10,11... | collective-permute-start | bytes 491528 | tf_op jit(solution)/shard_map/ppermute | solution.py:220
  89.0 15.3 %collective-permute-start.4 = (bf16[128,512]{1,0:T(8,128)(2,1)S(1)}, bf16[128,512]{1,0:T(8,128)(2,1)S(1)}, u32[]{:S(2)}, u32[]{:S(2)}) collective-permute-start(bf16[128,512]{1,0:T(8,128)(2,1)S(1)} %collective-permute-done.3.refs_2_), channel_id=1, source_target_pairs={{0,1},{1,0},{2,3},{3,2},{4,5},{5,4},{6,7},{7,6},{8,9},{9,8},{10,11... | collective-permute-start | bytes 393224 | tf_op jit(solution)/shard_map/ppermute | solution.py:220
  89.1 15.1 %collective-permute-start.5 = (bf16[64,512]{1,0:T(8,128)(2,1)S(1)}, bf16[64,512]{1,0:T(8,128)(2,1)S(1)}, u32[]{:S(2)}, u32[]{:S(2)}) collective-permute-start(bf16[64,512]{1,0:T(8,128)(2,1)S(1)} %add_convert_fusion.8.refs_0_), channel_id=1, source_target_pairs={{0,3},{1,2},{2,1},{3,0},{4,7},{5,6},{6,5},{7,4},{8,11},{9,10},{10,... | collective-permute-start | bytes 196616 | tf_op jit(solution)/shard_map/ppermute | solution.py:217
  90.5 13.7 %collective-permute-start.6 = (bf16[64,512]{1,0:T(8,128)(2,1)S(1)}, bf16[64,512]{1,0:T(8,128)(2,1)S(1)}, u32[]{:S(2)}, u32[]{:S(2)}) collective-permute-start(bf16[64,512]{1,0:T(8,128)(2,1)S(1)} %add_convert_fusion.8.refs_0_), channel_id=1, source_target_pairs={{0,2},{1,3},{2,0},{3,1},{4,6},{5,7},{6,4},{7,5},{8,10},{9,11},{10,... | collective-permute-start | bytes 196616 | tf_op jit(solution)/shard_map/ppermute | solution.py:214
